TPU v7x, 256 devices: a whole 4x4x8 slice. The times are simulated.
256 devices in a mesh: row: 32 (over x, z_hi, core), col: 8 (over z_lo, y).
Axes of the slice: x: 4, y: 4, z: 8 (z_hi: 4, z_lo: 2; z = z_hi * 2 + z_lo), core: 2. Of those that a mesh axis runs over, the one named last changes fastest.
Arguments:
- amplitudes: float32 [32, 8, 1024, 1024], P('row', 'col'), may hold values from -6 to 6
- panels_left: bfloat16 [32, 2, 1024, 1024], P('row', None, 'col'), may hold values from -6 to 6
- panels_right: bfloat16 [8, 2, 1024, 1024], P('col', None, 'row'), may hold values from -6 to 6
- weights_right: bfloat16 [2, 8, 1024, 1024], P(None, 'col', 'row'), may hold values from -0.125 to 0.125
- weights_left: bfloat16 [2, 32, 1024, 1024], P(None, 'row', 'col'), may hold values from -0.125 to 0.125
- energy_left: float32 [32], P('row'), may hold values from -2 to -0.5
- energy_right: float32 [8], P('col'), may hold values from -2 to -0.5
- energy_virtual: float32 [1024], replicated, may hold values from 0.5 to 3
Outputs:
- updated: float32 [32, 8, 1024, 1024], P('row', 'col')
All inputs are finite; a program needn't handle non-finite values.
Results may differ from a plain program's by a relative error of at most 0.0018.
Values may be sent and summed in bfloat16 or wider, within the bound.
A program may use at most 128 MiB of HBM per device.

v0:
```python
import jax
import jax.numpy as jnp
from jax import lax
from jax.sharding import PartitionSpec as P


def combine_blocks(blocks):
    as_float = blocks.astype(jnp.float32)
    return (2.0 * as_float - jnp.swapaxes(as_float, -1, -2)).astype(jnp.bfloat16)


def body(
    amplitudes,
    panels_left,
    panels_right,
    weights_right,
    weights_left,
    energy_left,
    energy_right,
    energy_virtual,
):
    left_slab = panels_left[0]
    right_slab = panels_right[0]
    right_weight_slab = weights_right[:, 0]
    left_weight_slab = weights_left[:, 0]
    left_whole = lax.all_gather(left_slab, "col", axis=1, tiled=True)
    left_mixed = combine_blocks(left_whole)
    mixed_cols = left_mixed
    direct = jnp.einsum(
        "kac,kcb->ab",
        mixed_cols,
        lax.all_gather(right_weight_slab, "row", axis=1, tiled=True),
        preferred_element_type=jnp.float32,
    )
    right_whole = lax.all_gather(right_slab, "row", axis=1, tiled=True)
    right_mixed = combine_blocks(right_whole)
    mixed_cols = right_mixed
    mirror = jnp.einsum(
        "kac,kcb->ab",
        mixed_cols,
        lax.all_gather(left_weight_slab, "col", axis=1, tiled=True),
        preferred_element_type=jnp.float32,
    )
    residual = direct + jnp.transpose(mirror)
    virt_pair = energy_virtual[:, None] + energy_virtual[None, :]
    denominator = energy_left[0] + energy_right[0] - virt_pair
    return (amplitudes[0, 0] + residual / denominator)[None, None]


def solution(mesh):
    placed = (
        P("row", "col", None, None),
        P("row", None, "col", None),
        P("col", None, "row", None),
        P(None, "col", "row", None),
        P(None, "row", "col", None),
        P("row"),
        P("col"),
        P(),
    )
    return jax.shard_map(
        body, mesh=mesh, in_specs=placed, out_specs=P("row", "col", None, None), check_vma=False
    )
```

profile of v0, /device:TPU:1, one launch (start us, length us, event | category | flops | bytes accessed | tf_op | source)
XLA Modules:
  0.0 267.6 jit_solution(162221997629663721)
XLA Ops:
  6.5 0.0 all-gather.9.cloned.1.call-start
  6.5 0.7 all-gather.9.cloned.1.call-update
  7.3 0.0 all-gather.13.cloned.1.call-start
  7.3 0.7 all-gather.13.cloned.1.call-update
  8.0 0.0 all-gather.11.cloned.1.call-start
  8.1 0.7 all-gather.11.cloned.1.call-update
  8.7 0.0 all-gather.15.cloned.1.call-start
  8.8 0.5 all-gather.15.cloned.1.call-update
  10.6 57.3 %all-gather.9.cloned.1.call-done = bf16[1,2,1024,1024]{3,2,1,0:T(8,128)(2,1)} async-done(((bf16[1,2,128,1024]{3,2,1,0:T(8,128)(2,1)}), bf16[1,2,1024,1024]{3,2,1,0:T(8,128)(2,1)}) %all-gather.9.cloned.1.call-update) | async-done | bytes 4194320 | tf_op jit(solution)/shard_map/all_gather | solution.py:26
  68.0 6.5 %bitcast_convert_fusion.1 = f32[2,1024,1024]{2,1,0:T(8,128)} fusion(bf16[1,2,1024,1024]{3,2,1,0:T(8,128)(2,1)} %all-gather.9.cloned.1.call-done), kind=kLoop, calls=%fused_computation.13 | loop fusion | flops 2097152 | bytes 12582912 | tf_op jit(solution)/shard_map/convert_element_type | solution.py:8
  74.4 8.7 %copy.9 = f32[2,1024,1024]{1,2,0:T(8,128)} copy(f32[2,1024,1024]{2,1,0:T(8,128)} %bitcast_convert_fusion.1) | data formatting | bytes 16777216 | tf_op jit(solution)/shard_map/convert_element_type | solution.py:8
  83.1 47.2 %all-gather.13.cloned.1.call-done = bf16[1,2,1024,1024]{3,2,1,0:T(8,128)(2,1)} async-done(((bf16[1,2,32,1024]{3,2,1,0:T(8,128)(2,1)}), bf16[1,2,1024,1024]{3,2,1,0:T(8,128)(2,1)}) %all-gather.13.cloned.1.call-update) | async-done | bytes 4194320 | tf_op jit(solution)/shard_map/all_gather | solution.py:35
  130.2 6.5 %bitcast_convert_fusion = f32[2,1024,1024]{2,1,0:T(8,128)} fusion(bf16[1,2,1024,1024]{3,2,1,0:T(8,128)(2,1)} %all-gather.13.cloned.1.call-done), kind=kLoop, calls=%fused_computation.11 | loop fusion | flops 2097152 | bytes 12582912 | tf_op jit(solution)/shard_map/convert_element_type | solution.py:8
  136.7 8.7 %copy.12 = f32[2,1024,1024]{1,2,0:T(8,128)} copy(f32[2,1024,1024]{2,1,0:T(8,128)} %bitcast_convert_fusion) | data formatting | bytes 16777216 | tf_op jit(solution)/shard_map/convert_element_type | solution.py:8
  145.4 0.0 copy-start
  145.4 45.9 %all-gather.11.cloned.1.call-done = bf16[2,1,1024,1024]{3,2,0,1:T(8,128)(2,1)} async-done(((bf16[2,1,32,1024]{3,2,0,1:T(8,128)(2,1)}), bf16[2,1,1024,1024]{3,2,0,1:T(8,128)(2,1)}) %all-gather.11.cloned.1.call-update) | async-done | bytes 4194320 | tf_op jit(solution)/shard_map/all_gather | solution.py:32
  191.4 12.6 %fusion.2 = f32[1024,1024,1]{1,0,2:T(8,128)} fusion(f32[2,1024,1024]{1,2,0:T(8,128)} %copy.9, bf16[2,1,1024,1024]{3,2,0,1:T(8,128)(2,1)} %all-gather.11.cloned.1.call-done, bf16[1,2,1024,1024]{3,2,1,0:T(8,128)(2,1)} %all-gather.9.cloned.1.call-done), kind=kOutput, calls=%fused_computation.4 | convolution fusion | flops 4303355904 | bytes 20971520 | tf_op jit(solution)/shard_map/kac,kcb->ab/dot_general | solution.py:29
  204.0 41.8 %all-gather.15.cloned.1.call-done = bf16[2,1,1024,1024]{3,2,0,1:T(8,128)(2,1)} async-done(((bf16[2,1,128,1024]{3,2,0,1:T(8,128)(2,1)}), bf16[2,1,1024,1024]{3,2,0,1:T(8,128)(2,1)}) %all-gather.15.cloned.1.call-update) | async-done | bytes 4194320 | tf_op jit(solution)/shard_map/all_gather | solution.py:41
  245.8 0.0 copy-done
  245.8 15.3 %fusion.8 = f32[1,1,1024,1024]{3,2,1,0:T(8,128)} fusion(f32[1024,1024,1]{1,0,2:T(8,128)} %fusion.2, f32[1,1,1024,1024]{3,2,1,0:T(8,128)} %param.8, f32[1024]{0:T(1024)S(1)} %copy-done, f32[]{:T(128)} %bitcast.14, bf16[2,1,1024,1024]{3,2,0,1:T(8,128)(2,1)} %all-gather.15.cloned.1.call-done, f32[2,1024,1024]{1,2,0:T(8,128)} %copy.12, ...), kind=kOutput, calls=%fused_computation.9 | convolution fusion | flops 4308598784 | bytes 29364228 | tf_op jit(solution)/shard_map/kac,kcb->ab/dot_general | solution.py:38
Async XLA Ops:
  6.5 61.4 %all-gather.9.cloned.1.call-start = ((), (), s32[]{:S(2)}) async-start(), calls=%async_computation | async-start | bytes 4718592 | tf_op jit(solution)/shard_map/all_gather | solution.py:26
  7.3 123.0 %all-gather.13.cloned.1.call-start = ((), (), s32[]{:S(2)}) async-start(), calls=%async_computation.2 | async-start | bytes 4325376 | tf_op jit(solution)/shard_map/all_gather | solution.py:35
  8.0 183.4 %all-gather.11.cloned.1.call-start = ((), (), s32[]{:S(2)}) async-start(), calls=%async_computation.1 | async-start | bytes 4325376 | tf_op jit(solution)/shard_map/all_gather | solution.py:32
  8.7 237.0 %all-gather.15.cloned.1.call-start = ((), (), s32[]{:S(2)}) async-start(), calls=%async_computation.3 | async-start | bytes 4718592 | tf_op jit(solution)/shard_map/all_gather | solution.py:41
  145.4 100.3 %copy-start = (f32[1024]{0:T(1024)S(1)}, f32[1024]{0:T(1024)}, u32[]{:S(2)}) copy-start(f32[1024]{0:T(1024)} %param.15) | copy-start | bytes 12292
Sparse Core Ops, SparseCore 0:
  9.1 58.7 all-gather.8
  70.6 59.5 all-gather.12
  132.9 58.4 all-gather.10
  193.0 52.7 all-gather.14
where the time goes:
time: 268 us
  waiting for transfers between devices  195 us (73%)
  matrix products  27.9 us (10%)
  local copies, waits for them, and re-layouts  17.4 us (6%)
  between operations  14.4 us (5%)
  other arithmetic  12.9 us (5%)
    all_gather x1, waiting for transfers between devices, body(): left_whole = lax.all_gather(left_slab, 'col', axis=1, tiled=True)  57.3 us
    all_gather x1, waiting for transfers between devices, body(): right_whole = lax.all_gather(right_slab, 'row', axis=1, tiled=True)  47.2 us
    all_gather x1, waiting for transfers between devices, body(): lax.all_gather(right_weight_slab, 'row', axis=1, tiled=True)  45.9 us
    all_gather x1, waiting for transfers between devices, body(): lax.all_gather(left_weight_slab, 'col', axis=1, tiled=True)  41.8 us
    convert_element_type x2, local copies, waits for them, and re-layouts, combine_blocks(): as_float = blocks.astype(jnp.float32)  17.4 us
    dot_general x1, matrix products, body(): jnp.einsum('kac,kcb->ab', mixed_cols, lax.all_gather(left_weight_slab, 'c...  15.3 us
    convert_element_type x2, other arithmetic, combine_blocks(): as_float = blocks.astype(jnp.float32)  12.9 us
    dot_general x1, matrix products, body(): jnp.einsum('kac,kcb->ab', mixed_cols, lax.all_gather(right_weight_slab, '...  12.6 us
  transfers between devices with their start and end apart: 4, of which 4 were waited for; matrix products, arithmetic and copies ran while one was open for 16% of the time, Pallas kernels for 0%

commit v1 on v0

--- a/solution.py
+++ b/solution.py
@@ -23,7 +23,7 @@
     right_slab = panels_right[0]
     right_weight_slab = weights_right[:, 0]
     left_weight_slab = weights_left[:, 0]
-    left_whole = lax.all_gather(left_slab, "col", axis=1, tiled=True)
+    left_whole = jnp.concatenate(lax.all_gather(left_slab, "col"), axis=1)
     left_mixed = combine_blocks(left_whole)
     mixed_cols = left_mixed
     direct = jnp.einsum(

time: 268 us -> 267 us (level)
  other arithmetic: 12.9 us -> 23 us
  waiting for transfers between devices: 195 us -> 186 us
    all_gather x1, waiting for transfers between devices: 47.2 us -> 37.1 us  [body(): right_whole = lax.all_gather(right_slab, 'row', axis=1, tiled=True)]
    convert_element_type x0 -> x1, other arithmetic: none -> 10 us  [combine_blocks(): (2.0 * as_float - jnp.swapaxes(as_float, -1, -2)).astype(jnp.bfloat16)]
    all_gather x1, waiting for transfers between devices: 45.9 us -> 49.7 us  [body(): lax.all_gather(right_weight_slab, 'row', axis=1, tiled=True)]
    dot_general x1, matrix products: 15.3 us -> 12.4 us  [body(): jnp.einsum('kac,kcb->ab', mixed_cols, lax.all_gather(left_weight_slab, 'c...]
  transfers between devices with their start and end apart: 4 -> 4, of which waited for: 4 -> 4; matrix products, arithmetic and copies ran while one was open for 16% -> 20% of each run, Pallas kernels for 0% -> 0%
where the time goes in v1:
time: 267 us; the launch traced here: 266 us
  waiting for transfers between devices  186 us (70%)
  matrix products  25.3 us (9%)
  other arithmetic  23 us (9%)
  local copies, waits for them, and re-layouts  17.4 us (7%)
  between operations  14.4 us (5%)
    all_gather x1, waiting for transfers between devices, body(): left_whole = jnp.concatenate(lax.all_gather(left_slab, 'col'), axis=1)  57.3 us
    all_gather x1, waiting for transfers between devices, body(): lax.all_gather(right_weight_slab, 'row', axis=1, tiled=True)  49.7 us
    all_gather x1, waiting for transfers between devices, body(): lax.all_gather(left_weight_slab, 'col', axis=1, tiled=True)  39.3 us
    all_gather x1, waiting for transfers between devices, body(): right_whole = lax.all_gather(right_slab, 'row', axis=1, tiled=True)  37.1 us
    convert_element_type x2, local copies, waits for them, and re-layouts, combine_blocks(): as_float = blocks.astype(jnp.float32)  17.4 us
    convert_element_type x2, other arithmetic, combine_blocks(): as_float = blocks.astype(jnp.float32)  12.9 us
    dot_general x1, matrix products, body(): jnp.einsum('kac,kcb->ab', mixed_cols, lax.all_gather(right_weight_slab, '...  12.9 us
    dot_general x1, matrix products, body(): jnp.einsum('kac,kcb->ab', mixed_cols, lax.all_gather(left_weight_slab, 'c...  12.4 us
  transfers between devices with their start and end apart: 4, of which 4 were waited for; matrix products, arithmetic and copies ran while one was open for 20% of the time, Pallas kernels for 0%

profile of v1, /device:TPU:1, one launch (start us, length us, event | category | flops | bytes accessed | tf_op | source)
XLA Modules:
  0.0 266.4 jit_solution(4692943343791728522)
XLA Ops:
  6.5 0.0 all-gather.8.cloned.1.call-start
  6.5 0.7 all-gather.8.cloned.1.call-update
  7.3 0.0 all-gather.12.cloned.1.call-start
  7.3 0.7 all-gather.12.cloned.1.call-update
  8.0 0.0 all-gather.14.cloned.1.call-start
  8.1 0.7 all-gather.14.cloned.1.call-update
  8.7 0.0 all-gather.10.cloned.1.call-start
  8.8 0.5 all-gather.10.cloned.1.call-update
  10.6 57.3 %all-gather.8.cloned.1.call-done = bf16[8,2,128,1024]{3,2,1,0:T(8,128)(2,1)} async-done(((bf16[1,2,128,1024]{3,2,1,0:T(8,128)(2,1)}), bf16[8,2,128,1024]{3,2,1,0:T(8,128)(2,1)}) %all-gather.8.cloned.1.call-update) | async-done | bytes 4194320 | tf_op jit(solution)/shard_map/all_gather | solution.py:26
  67.9 6.5 %copy_convert_fusion = f32[8,2,128,1024]{3,2,0,1:T(8,128)} fusion(bf16[8,2,128,1024]{3,2,1,0:T(8,128)(2,1)} %all-gather.8.cloned.1.call-done), kind=kLoop, calls=%fused_computation.13 | loop fusion | flops 2097152 | bytes 12582912 | tf_op jit(solution)/shard_map/convert_element_type | solution.py:8
  74.4 8.7 %copy.25 = f32[2,1024,1024]{1,2,0:T(8,128)} copy(f32[2,1024,1024]{2,1,0:T(8,128)} %bitcast.47) | data formatting | bytes 16777216 | tf_op jit(solution)/shard_map/convert_element_type | solution.py:8
  83.1 10.0 %fusion = bf16[2,1024,1024]{1,2,0:T(8,128)(2,1)} fusion(f32[8,2,128,1024]{3,2,0,1:T(8,128)} %copy_convert_fusion, f32[2,1024,1024]{1,2,0:T(8,128)} %copy.25), kind=kLoop, calls=%fused_computation.1 | loop fusion | flops 6291456 | bytes 20971520 | tf_op jit(solution)/shard_map/convert_element_type | solution.py:9
  93.1 37.1 %all-gather.12.cloned.1.call-done = bf16[1,2,1024,1024]{3,2,1,0:T(8,128)(2,1)} async-done(((bf16[1,2,32,1024]{3,2,1,0:T(8,128)(2,1)}), bf16[1,2,1024,1024]{3,2,1,0:T(8,128)(2,1)}) %all-gather.12.cloned.1.call-update) | async-done | bytes 4194320 | tf_op jit(solution)/shard_map/all_gather | solution.py:35
  130.2 6.5 %bitcast_convert_fusion = f32[2,1024,1024]{2,1,0:T(8,128)} fusion(bf16[1,2,1024,1024]{3,2,1,0:T(8,128)(2,1)} %all-gather.12.cloned.1.call-done), kind=kLoop, calls=%fused_computation.10 | loop fusion | flops 2097152 | bytes 12582912 | tf_op jit(solution)/shard_map/convert_element_type | solution.py:8
  136.7 8.7 %copy.28 = f32[2,1024,1024]{1,2,0:T(8,128)} copy(f32[2,1024,1024]{2,1,0:T(8,128)} %bitcast_convert_fusion) | data formatting | bytes 16777216 | tf_op jit(solution)/shard_map/convert_element_type | solution.py:8
  145.5 0.0 copy-start
  145.5 39.3 %all-gather.14.cloned.1.call-done = bf16[2,1,1024,1024]{3,2,0,1:T(8,128)(2,1)} async-done(((bf16[2,1,128,1024]{3,2,0,1:T(8,128)(2,1)}), bf16[2,1,1024,1024]{3,2,0,1:T(8,128)(2,1)}) %all-gather.14.cloned.1.call-update) | async-done | bytes 4194320 | tf_op jit(solution)/shard_map/all_gather | solution.py:41
  184.8 12.4 %fusion.2 = f32[1024,1024,1]{0,1,2:T(8,128)} fusion(f32[2,1024,1024]{1,2,0:T(8,128)} %copy.28, bf16[2,1,1024,1024]{3,2,0,1:T(8,128)(2,1)} %all-gather.14.cloned.1.call-done, bf16[1,2,1024,1024]{3,2,1,0:T(8,128)(2,1)} %all-gather.12.cloned.1.call-done), kind=kOutput, calls=%fused_computation.4 | convolution fusion | flops 4303355904 | bytes 20971520 | tf_op jit(solution)/shard_map/kac,kcb->ab/dot_general | solution.py:38
  197.2 49.7 %all-gather.10.cloned.1.call-done = bf16[2,1,1024,1024]{3,2,0,1:T(8,128)(2,1)} async-done(((bf16[2,1,32,1024]{3,2,0,1:T(8,128)(2,1)}), bf16[2,1,1024,1024]{3,2,0,1:T(8,128)(2,1)}) %all-gather.10.cloned.1.call-update) | async-done | bytes 4194320 | tf_op jit(solution)/shard_map/all_gather | solution.py:32
  246.9 0.0 copy-done
  246.9 12.9 %fusion.6 = f32[1,1,1024,1024]{3,2,1,0:T(8,128)} fusion(f32[1024,1024,1]{0,1,2:T(8,128)} %fusion.2, f32[1,1,1024,1024]{3,2,1,0:T(8,128)} %param.8, f32[1024]{0:T(1024)S(1)} %copy-done, f32[]{:T(128)} %bitcast.15, bf16[2,1024,1024]{1,2,0:T(8,128)(2,1)} %fusion, bf16[2,1,1024,1024]{3,2,0,1:T(8,128)(2,1)} %all-gather.10.cloned.1.call-done), kind=kOutput, calls=%fused_computation.8 | convolution fusion | flops 4300210176 | bytes 20975620 | tf_op jit(solution)/shard_map/kac,kcb->ab/dot_general | solution.py:29
Async XLA Ops:
  6.5 61.4 %all-gather.8.cloned.1.call-start = ((), (), s32[]{:S(2)}) async-start(), calls=%async_computation | async-start | bytes 4718592 | tf_op jit(solution)/shard_map/all_gather | solution.py:26
  7.3 123.0 %all-gather.12.cloned.1.call-start = ((), (), s32[]{:S(2)}) async-start(), calls=%async_computation.2 | async-start | bytes 4325376 | tf_op jit(solution)/shard_map/all_gather | solution.py:35
  8.0 176.8 %all-gather.14.cloned.1.call-start = ((), (), s32[]{:S(2)}) async-start(), calls=%async_computation.3 | async-start | bytes 4718592 | tf_op jit(solution)/shard_map/all_gather | solution.py:41
  8.7 238.2 %all-gather.10.cloned.1.call-start = ((), (), s32[]{:S(2)}) async-start(), calls=%async_computation.1 | async-start | bytes 4325376 | tf_op jit(solution)/shard_map/all_gather | solution.py:32
  145.5 101.5 %copy-start = (f32[1024]{0:T(1024)S(1)}, f32[1024]{0:T(1024)}, u32[]{:S(2)}) copy-start(f32[1024]{0:T(1024)} %param.15) | copy-start | bytes 12292
Sparse Core Ops, SparseCore 0:
  9.1 58.7 all-gather.7
  70.6 59.5 all-gather.11
  132.0 52.7 all-gather.13
  187.3 59.5 all-gather.9
